TPU v7x, 32 devices: a whole 2x2x4 slice. The times are simulated.
32 devices in a mesh: wav: 8 (over y, x, core), lev: 4 (over z).
Axes of the slice: x: 2, y: 2, z: 4, core: 2. Of those that a mesh axis runs over, the one named last changes fastest.
Arguments:
- spectral: bfloat16 [200, 401, 512], P('wav', None, 'lev'), may hold values from -0.1796875 to 0.1796875
- legendre: bfloat16 [200, 401, 64], P('wav', None, 'lev'), may hold values from -0.4375 to 0.4375
- wave_pair: int32 [200], replicated, may hold values from -1 to 199, as said below
- lat_slot: int32 [64], replicated, may hold values from 0 to 799, as said below
Outputs:
- gridded: bfloat16 [64, 256, 1616], P('wav', 'lev')
Inputs may be any that keep to these rules, and one draw needn't show every extreme that they name: `wave_pair`: each pair number 0 to 199 appears exactly once; all other entries are -1. `lat_slot`: the entries are distinct latitudes.
All inputs are finite; a program needn't handle non-finite values.
Results may differ from a plain program's by a relative error of at most 0.0055.
Values may be sent and summed in bfloat16 or wider, within the bound.
A program may use at most 64 MiB of HBM per device.

v0:
```python
import math
import jax
import jax.numpy as jnp
from jax import lax
from jax.sharding import PartitionSpec as P

NLAT = 800


def fold_masks(pair_ids, fold_count, wave_count):
    fold_rows = jnp.arange(fold_count, dtype=jnp.int32)
    filled = pair_ids >= 0
    border = wave_count - pair_ids
    lower = filled[:, None] & (fold_rows[None, :] < border[:, None])
    upper = filled[:, None] & (fold_rows[None, :] >= border[:, None])
    return jnp.stack([lower, upper], axis=1)


def trig_parts(wave_numbers, steps, counts_b):
    residue = wave_numbers[None, None] * steps[None, :, None, None] % counts_b
    angles = residue.astype(jnp.float32) * (2.0 * math.pi) / counts_b.astype(jnp.float32)
    return (jnp.cos(angles), jnp.sin(angles))


def synthesis_table(pair_ids, row_lats, lat_count, lon_width, wave_count):
    filled = pair_ids >= 0
    wave_numbers = jnp.stack([pair_ids, wave_count - 1 - pair_ids], axis=1)
    lon_count = 20 + 4 * jnp.minimum(row_lats, lat_count - 1 - row_lats)
    highest = jnp.minimum(wave_count - 1, (lon_count - 1) // 2)
    counts_b = lon_count[:, None, None, None]
    coarse_count = (lon_width + 63) // 64
    coarse_steps = jnp.arange(coarse_count, dtype=jnp.int32) * 64
    fine_steps = jnp.arange(64, dtype=jnp.int32)
    cos_coarse, sin_coarse = trig_parts(wave_numbers, coarse_steps, counts_b)
    cos_fine, sin_fine = trig_parts(wave_numbers, fine_steps, counts_b)
    cos_all = (
        cos_coarse[:, :, None] * cos_fine[:, None] - sin_coarse[:, :, None] * sin_fine[:, None]
    )
    sin_all = (
        sin_coarse[:, :, None] * cos_fine[:, None] + cos_coarse[:, :, None] * sin_fine[:, None]
    )
    row_total = row_lats.shape[0]
    cos_all = cos_all.reshape(row_total, coarse_count * 64, wave_numbers.shape[0], 2)[:, :lon_width]
    sin_all = sin_all.reshape(row_total, coarse_count * 64, wave_numbers.shape[0], 2)[:, :lon_width]
    columns = jnp.arange(lon_width, dtype=jnp.int32)
    valid = (
        filled[None, None, :, None]
        & (wave_numbers[None, None] <= highest[:, None, None, None])
        & (columns[None, :, None, None] < counts_b)
    )
    factor = jnp.where(wave_numbers == 0, 1.0, 2.0).astype(jnp.float32)[None, None]
    real_part = jnp.where(valid, factor * cos_all, 0.0)
    imag_part = jnp.where(valid, -factor * sin_all, 0.0)
    return jnp.stack([real_part, imag_part], axis=-1).astype(jnp.bfloat16)


def legendre_sum(coefficients, weights, half_masks):
    paired = coefficients.reshape(
        coefficients.shape[0], coefficients.shape[1], coefficients.shape[2] // 2, 2
    )
    masked = jnp.where(
        half_masks[:, :, :, None, None], paired[:, None], jnp.zeros((), paired.dtype)
    )
    summed = jnp.einsum("shtlc,sta->ashcl", masked, weights, preferred_element_type=jnp.float32)
    return summed.astype(jnp.bfloat16)


def on_device(spectral, legendre, wave_pair, lat_slot):
    slot_count = spectral.shape[0]
    fold_count = spectral.shape[1]
    wave_count = fold_count - 1
    lat_count = NLAT
    lon_width = 2 * lat_count + 16
    wav_devices = lax.axis_size("wav")
    wav_index = lax.axis_index("wav")
    own_pairs = lax.dynamic_slice_in_dim(wave_pair, wav_index * slot_count, slot_count)
    half_masks = fold_masks(own_pairs, fold_count, wave_count)
    fourier = legendre_sum(
        spectral, lax.all_gather(legendre, "lev", axis=2, tiled=True), half_masks
    )
    row_count = lat_slot.shape[0] // wav_devices
    row_lats = lax.dynamic_slice_in_dim(lat_slot, wav_index * row_count, row_count)
    group_rows = max(1, row_count // 25)
    while row_count % group_rows:
        group_rows -= 1
    group_count = row_count // group_rows
    received = lax.all_to_all(fourier, "wav", split_axis=0, concat_axis=1, tiled=True)
    layer_items = received.shape[4]
    grouped = received.reshape((group_count, group_rows) + received.shape[1:])
    lat_groups = row_lats.reshape(group_count, group_rows)

    def one_group(args):
        values, group_lats = args
        basis = synthesis_table(wave_pair, group_lats, lat_count, lon_width, wave_count)
        result = jnp.einsum("rjghc,rghcl->rlj", basis, values, preferred_element_type=jnp.float32)
        return result.astype(jnp.bfloat16)

    gridded_groups = lax.map(one_group, (grouped, lat_groups))
    return gridded_groups.reshape(row_count, layer_items, lon_width)


def solution(mesh):
    return jax.shard_map(
        on_device,
        mesh=mesh,
        in_specs=(P("wav", None, "lev"), P("wav", None, "lev"), P(), P()),
        out_specs=P("wav", "lev", None),
        check_vma=False,
    )
```

profile of v0, /device:TPU:0, one launch (start us, length us, event | category | flops | bytes accessed | tf_op | source)
XLA Modules:
  0.0 257.9 jit_solution(4773059625746741273)
XLA Ops:
  7.3 5.4 %copy.16 = bf16[25,401,128]{1,2,0:T(8,128)(2,1)} copy(bf16[25,401,128]{2,1,0:T(8,128)(2,1)} %param.6) | data formatting | bytes 5132800 | tf_op args[0]
  12.7 6.7 %broadcast_in_dim.92 = bf16[25,401,64,2]{1,3,2,0:T(2,128)(2,1)S(1)} reshape(bf16[25,401,128]{1,2,0:T(8,128)(2,1)} %copy.16) | data formatting | bytes 5132800 | tf_op jit(solution)/shard_map/jit(_where)/broadcast_in_dim | solution.py:61
  22.3 27.4 %all-gather.2.cloned.1.call-done = bf16[25,401,64]{1,2,0:T(8,128)(2,1)} async-done(((bf16[25,401,16]{1,2,0:T(8,128)(2,1)}), bf16[25,401,64]{1,2,0:T(8,128)(2,1)}) %all-gather.2.cloned.1.call-update) | async-done | bytes 1283216 | tf_op jit(solution)/shard_map/all_gather | solution.py:79
  49.8 4.3 %fusion.52 = bf16[64,25,2,2,64]{0,4,3,2,1:T(8,128)(2,1)S(1)} fusion(bf16[25,401,64]{1,2,0:T(8,128)(2,1)} %all-gather.2.cloned.1.call-done, pred[25,2,401]{2,1,0:T(4,128)(4,1)S(1)} %pad_add_fusion.1, bf16[25,401,64,2]{1,2,3,0:T(8,128)(2,1)} %copy.17), kind=kOutput, calls=%fused_computation.59 | convolution fusion | flops 331475200 | bytes 4688850 | tf_op jit(solution)/shard_map/shtlc,sta->ashcl/dot_general | solution.py:64
  54.0 3.0 %copy.18 = bf16[64,25,2,2,64]{4,3,2,1,0:T(2,128)(2,1)S(1)} copy(bf16[64,25,2,2,64]{0,4,3,2,1:T(8,128)(2,1)S(1)} %fusion.52) | data formatting | bytes 1638400 | tf_op jit(solution)/shard_map/convert_element_type | solution.py:65
  58.9 3.7 %all-to-all-start = ((bf16[8,2,25600]{2,1,0:T(2,128)(2,1)}), bf16[8,2,25600]{2,1,0:T(2,128)(2,1)S(1)}, u32[]{:S(2)}, u32[]{:S(2)}) async-start(bf16[8,2,25600]{2,1,0:T(2,128)(2,1)} %reshape.584), calls=%async_computation | async-start | bytes 1638400 | tf_op jit(solution)/shard_map/all_to_all | solution.py:87
  62.7 12.7 %all-to-all-done = bf16[8,2,25600]{2,1,0:T(2,128)(2,1)S(1)} async-done(((bf16[8,2,25600]{2,1,0:T(2,128)(2,1)}), bf16[8,2,25600]{2,1,0:T(2,128)(2,1)S(1)}, u32[]{:S(2)}, u32[]{:S(2)}) %all-to-all-start) | async-done | bytes 819232 | tf_op jit(solution)/shard_map/all_to_all | solution.py:87
  79.6 171.5 %while.15 = (s32[]{:T(128)}, bf16[8,1,64,1616]{3,2,1,0:T(8,128)(2,1)}, bf16[8,1,200,2,2,64]{2,5,3,4,1,0:T(8,128)(2,1)}, s32[200]{0:T(256)S(1)}, s32[8,1]{0,1:T(1...) while((s32[]{:T(128)}, ...), condition=%wide.region_1.2_spmd, body=%wide.region_0.1_spmd.sunk | while | flops 175794288 | bytes 47638996 | solution.py:98
  87.0 3.5 %copy.30 = f32[1,1616,200,2]{1,2,3,0:T(8,128)} copy(f32[1,1616,200,2]{2,1,3,0:T(8,128)} %slice.24) | data formatting | bytes 5171200 | tf_op jit(solution)/shard_map/while
  92.4 3.7 %copy.31 = f32[1,1616,200,2]{1,2,3,0:T(8,128)} copy(f32[1,1616,200,2]{2,1,3,0:T(8,128)} %slice.25) | data formatting | bytes 5171200 | tf_op jit(solution)/shard_map/while
  96.2 2.5 fusion.68
  108.4 3.5 %copy.30 = f32[1,1616,200,2]{1,2,3,0:T(8,128)} copy(f32[1,1616,200,2]{2,1,3,0:T(8,128)} %slice.24) | data formatting | bytes 5171200 | tf_op jit(solution)/shard_map/while
  113.8 3.7 %copy.31 = f32[1,1616,200,2]{1,2,3,0:T(8,128)} copy(f32[1,1616,200,2]{2,1,3,0:T(8,128)} %slice.25) | data formatting | bytes 5171200 | tf_op jit(solution)/shard_map/while
  117.6 2.5 fusion.68
  129.8 3.5 %copy.30 = f32[1,1616,200,2]{1,2,3,0:T(8,128)} copy(f32[1,1616,200,2]{2,1,3,0:T(8,128)} %slice.24) | data formatting | bytes 5171200 | tf_op jit(solution)/shard_map/while
  135.3 3.7 %copy.31 = f32[1,1616,200,2]{1,2,3,0:T(8,128)} copy(f32[1,1616,200,2]{2,1,3,0:T(8,128)} %slice.25) | data formatting | bytes 5171200 | tf_op jit(solution)/shard_map/while
  139.1 2.5 fusion.68
  151.3 3.5 %copy.30 = f32[1,1616,200,2]{1,2,3,0:T(8,128)} copy(f32[1,1616,200,2]{2,1,3,0:T(8,128)} %slice.24) | data formatting | bytes 5171200 | tf_op jit(solution)/shard_map/while
  156.7 3.7 %copy.31 = f32[1,1616,200,2]{1,2,3,0:T(8,128)} copy(f32[1,1616,200,2]{2,1,3,0:T(8,128)} %slice.25) | data formatting | bytes 5171200 | tf_op jit(solution)/shard_map/while
  160.5 2.5 fusion.68
  172.7 3.5 %copy.30 = f32[1,1616,200,2]{1,2,3,0:T(8,128)} copy(f32[1,1616,200,2]{2,1,3,0:T(8,128)} %slice.24) | data formatting | bytes 5171200 | tf_op jit(solution)/shard_map/while
  178.1 3.7 %copy.31 = f32[1,1616,200,2]{1,2,3,0:T(8,128)} copy(f32[1,1616,200,2]{2,1,3,0:T(8,128)} %slice.25) | data formatting | bytes 5171200 | tf_op jit(solution)/shard_map/while
  181.9 2.5 fusion.68
  194.1 3.5 %copy.30 = f32[1,1616,200,2]{1,2,3,0:T(8,128)} copy(f32[1,1616,200,2]{2,1,3,0:T(8,128)} %slice.24) | data formatting | bytes 5171200 | tf_op jit(solution)/shard_map/while
  199.6 3.7 %copy.31 = f32[1,1616,200,2]{1,2,3,0:T(8,128)} copy(f32[1,1616,200,2]{2,1,3,0:T(8,128)} %slice.25) | data formatting | bytes 5171200 | tf_op jit(solution)/shard_map/while
  203.4 2.5 fusion.68
  215.6 3.5 %copy.30 = f32[1,1616,200,2]{1,2,3,0:T(8,128)} copy(f32[1,1616,200,2]{2,1,3,0:T(8,128)} %slice.24) | data formatting | bytes 5171200 | tf_op jit(solution)/shard_map/while
  221.0 3.7 %copy.31 = f32[1,1616,200,2]{1,2,3,0:T(8,128)} copy(f32[1,1616,200,2]{2,1,3,0:T(8,128)} %slice.25) | data formatting | bytes 5171200 | tf_op jit(solution)/shard_map/while
  224.8 2.5 fusion.68
  237.0 3.5 %copy.30 = f32[1,1616,200,2]{1,2,3,0:T(8,128)} copy(f32[1,1616,200,2]{2,1,3,0:T(8,128)} %slice.24) | data formatting | bytes 5171200 | tf_op jit(solution)/shard_map/while
  242.4 3.7 %copy.31 = f32[1,1616,200,2]{1,2,3,0:T(8,128)} copy(f32[1,1616,200,2]{2,1,3,0:T(8,128)} %slice.25) | data formatting | bytes 5171200 | tf_op jit(solution)/shard_map/while
  246.2 2.5 fusion.68
  (146 shorter events, 92.1 us)
Async XLA Ops:
  6.5 56.1 %copy-start = (s32[64]{0:T(128)S(1)}, s32[64]{0:T(128)}, u32[]{:S(2)}) copy-start(s32[64]{0:T(128)} %param.9) | copy-start | bytes 772
  6.5 43.2 %all-gather.2.cloned.1.call-start = ((), (), s32[]{:S(2)}) async-start(), calls=%async_computation.1 | async-start | bytes 2048000 | tf_op jit(solution)/shard_map/all_gather | solution.py:79
  19.4 2.4 copy-start.2
  58.9 16.6 %all-to-all-start = ((bf16[8,2,25600]{2,1,0:T(2,128)(2,1)}), bf16[8,2,25600]{2,1,0:T(2,128)(2,1)S(1)}, u32[]{:S(2)}, u32[]{:S(2)}) async-start(bf16[8,2,25600]{2,1,0:T(2,128)(2,1)} %reshape.584), calls=%async_computation | async-start | bytes 1638400 | tf_op jit(solution)/shard_map/all_to_all | solution.py:87
  92.4 3.8 %copy-start.1 = (f32[1,1616,200,2]{1,2,3,0:T(8,128)S(1)}, f32[1,1616,200,2]{1,2,3,0:T(8,128)}, u32[]{:S(2)}) copy-start(f32[1,1616,200,2]{1,2,3,0:T(8,128)} %copy.30) | copy-start | bytes 7756804 | tf_op jit(solution)/shard_map/while
  113.8 3.8 %copy-start.1 = (f32[1,1616,200,2]{1,2,3,0:T(8,128)S(1)}, f32[1,1616,200,2]{1,2,3,0:T(8,128)}, u32[]{:S(2)}) copy-start(f32[1,1616,200,2]{1,2,3,0:T(8,128)} %copy.30) | copy-start | bytes 7756804 | tf_op jit(solution)/shard_map/while
  135.3 3.8 %copy-start.1 = (f32[1,1616,200,2]{1,2,3,0:T(8,128)S(1)}, f32[1,1616,200,2]{1,2,3,0:T(8,128)}, u32[]{:S(2)}) copy-start(f32[1,1616,200,2]{1,2,3,0:T(8,128)} %copy.30) | copy-start | bytes 7756804 | tf_op jit(solution)/shard_map/while
  156.7 3.8 %copy-start.1 = (f32[1,1616,200,2]{1,2,3,0:T(8,128)S(1)}, f32[1,1616,200,2]{1,2,3,0:T(8,128)}, u32[]{:S(2)}) copy-start(f32[1,1616,200,2]{1,2,3,0:T(8,128)} %copy.30) | copy-start | bytes 7756804 | tf_op jit(solution)/shard_map/while
  178.1 3.8 %copy-start.1 = (f32[1,1616,200,2]{1,2,3,0:T(8,128)S(1)}, f32[1,1616,200,2]{1,2,3,0:T(8,128)}, u32[]{:S(2)}) copy-start(f32[1,1616,200,2]{1,2,3,0:T(8,128)} %copy.30) | copy-start | bytes 7756804 | tf_op jit(solution)/shard_map/while
  199.6 3.8 %copy-start.1 = (f32[1,1616,200,2]{1,2,3,0:T(8,128)S(1)}, f32[1,1616,200,2]{1,2,3,0:T(8,128)}, u32[]{:S(2)}) copy-start(f32[1,1616,200,2]{1,2,3,0:T(8,128)} %copy.30) | copy-start | bytes 7756804 | tf_op jit(solution)/shard_map/while
  221.0 3.8 %copy-start.1 = (f32[1,1616,200,2]{1,2,3,0:T(8,128)S(1)}, f32[1,1616,200,2]{1,2,3,0:T(8,128)}, u32[]{:S(2)}) copy-start(f32[1,1616,200,2]{1,2,3,0:T(8,128)} %copy.30) | copy-start | bytes 7756804 | tf_op jit(solution)/shard_map/while
  242.4 3.8 %copy-start.1 = (f32[1,1616,200,2]{1,2,3,0:T(8,128)S(1)}, f32[1,1616,200,2]{1,2,3,0:T(8,128)}, u32[]{:S(2)}) copy-start(f32[1,1616,200,2]{1,2,3,0:T(8,128)} %copy.30) | copy-start | bytes 7756804 | tf_op jit(solution)/shard_map/while
Sparse Core Ops, SparseCore 0:
  8.9 40.8 all-gather.1
where the time goes:
time: 259 us; the launch traced here: 258 us
  local copies, waits for them, and re-layouts  117 us (45%)
  other arithmetic  49.3 us (19%)
  waiting for transfers between devices  40.9 us (16%)
  matrix products  22.6 us (9%)
  between operations  13.5 us (5%)
  loops' own time  10.7 us (4%)
  starting transfers between devices  3.73 us (1%)
    while x32, local copies, waits for them, and re-layouts  58.4 us
    all_gather x1, waiting for transfers between devices, on_device(): lax.all_gather(legendre, 'lev', axis=2, tiled=True)  27.4 us
    cos x16, other arithmetic, trig_parts(): return (jnp.cos(angles), jnp.sin(angles))  22.2 us
    another operation x8, other arithmetic, synthesis_table(): return jnp.stack([real_part, imag_part], axis=-1).astype(jnp.bfloat16)  19.9 us
    dot_general x8, matrix products, one_group(): jnp.einsum('rjghc,rghcl->rlj', basis, values, preferred_element_type=jnp....  18.3 us
    slice x8, local copies, waits for them, and re-layouts, synthesis_table(): cos_all.reshape(row_total, coarse_count * 64, wave_numbers.shape[0], 2)  15.2 us
    slice x8, local copies, waits for them, and re-layouts, synthesis_table(): sin_all.reshape(row_total, coarse_count * 64, wave_numbers.shape[0], 2)  15.2 us
    all_to_all x1, waiting for transfers between devices, on_device(): lax.all_to_all(fourier, 'wav', split_axis=0, concat_axis=1, tiled=True)  12.7 us
  transfers between devices with their start and end apart: 2, of which 2 were waited for; matrix products, arithmetic and copies ran while one was open for 6% of the time, Pallas kernels for 0%

commit v1 on v0

--- a/solution.py
+++ b/solution.py
@@ -84,7 +84,10 @@
     while row_count % group_rows:
         group_rows -= 1
     group_count = row_count // group_rows
-    received = lax.all_to_all(fourier, "wav", split_axis=0, concat_axis=1, tiled=True)
+    received = jnp.concatenate(
+        lax.all_to_all(jnp.stack(jnp.split(fourier, lax.axis_size("wav"), axis=0)), "wav", 0, 0),
+        axis=1,
+    )
     layer_items = received.shape[4]
     grouped = received.reshape((group_count, group_rows) + received.shape[1:])
     lat_groups = row_lats.reshape(group_count, group_rows)

time: 259 us -> 257 us (level)
  local copies, waits for them, and re-layouts: 117 us -> 114 us
    convert_element_type x1 -> x0, local copies, waits for them, and re-layouts: 3 us -> none  [legendre_sum(): return summed.astype(jnp.bfloat16)]
    unnamed x7 -> x14, local copies, waits for them, and re-layouts: 8.24 us -> 8.73 us
where the time goes in v1:
time: 257 us; the launch traced here: 256 us
  local copies, waits for them, and re-layouts  114 us (44%)
  other arithmetic  49.3 us (19%)
  waiting for transfers between devices  40.9 us (16%)
  matrix products  24 us (9%)
  between operations  13.5 us (5%)
  loops' own time  10.7 us (4%)
  starting transfers between devices  3.73 us (1%)
    while x32, local copies, waits for them, and re-layouts  58.4 us
    all_gather x1, waiting for transfers between devices, on_device(): lax.all_gather(legendre, 'lev', axis=2, tiled=True)  27.4 us
    cos x16, other arithmetic, trig_parts(): return (jnp.cos(angles), jnp.sin(angles))  22.2 us
    another operation x8, other arithmetic, synthesis_table(): return jnp.stack([real_part, imag_part], axis=-1).astype(jnp.bfloat16)  19.9 us
    dot_general x8, matrix products, one_group(): jnp.einsum('rjghc,rghcl->rlj', basis, values, preferred_element_type=jnp....  18.3 us
    slice x8, local copies, waits for them, and re-layouts, synthesis_table(): cos_all.reshape(row_total, coarse_count * 64, wave_numbers.shape[0], 2)  15.2 us
    slice x8, local copies, waits for them, and re-layouts, synthesis_table(): sin_all.reshape(row_total, coarse_count * 64, wave_numbers.shape[0], 2)  15.2 us
    all_to_all x1, waiting for transfers between devices, on_device(): lax.all_to_all(jnp.stack(jnp.split(fourier, lax.axis_size('wav'), axis=0)...  12.7 us
  transfers between devices with their start and end apart: 2, of which 2 were waited for; matrix products, arithmetic and copies ran while one was open for 6% of the time, Pallas kernels for 0%

profile of v1, /device:TPU:0, one launch (start us, length us, event | category | flops | bytes accessed | tf_op | source)
XLA Modules:
  0.0 256.1 jit_solution(11682072765491706349)
XLA Ops:
  7.3 5.4 %copy.9 = bf16[25,401,128]{1,2,0:T(8,128)(2,1)} copy(bf16[25,401,128]{2,1,0:T(8,128)(2,1)} %param.6) | data formatting | bytes 5132800 | tf_op args[0]
  12.7 6.7 %broadcast_in_dim.92 = bf16[25,401,64,2]{1,3,2,0:T(2,128)(2,1)S(1)} reshape(bf16[25,401,128]{1,2,0:T(8,128)(2,1)} %copy.9) | data formatting | bytes 5132800 | tf_op jit(solution)/shard_map/jit(_where)/broadcast_in_dim | solution.py:61
  22.3 27.4 %all-gather.2.cloned.1.call-done = bf16[25,401,64]{1,2,0:T(8,128)(2,1)} async-done(((bf16[25,401,16]{1,2,0:T(8,128)(2,1)}), bf16[25,401,64]{1,2,0:T(8,128)(2,1)}) %all-gather.2.cloned.1.call-update) | async-done | bytes 1283216 | tf_op jit(solution)/shard_map/all_gather | solution.py:79
  49.8 5.7 %fusion.52 = bf16[64,25,2,2,64]{4,0,3,2,1:T(8,128)(2,1)S(1)} fusion(bf16[25,401,64]{1,2,0:T(8,128)(2,1)} %all-gather.2.cloned.1.call-done, pred[25,2,401]{2,1,0:T(4,128)(4,1)S(1)} %pad_add_fusion.1, bf16[25,401,64,2]{1,2,3,0:T(8,128)(2,1)} %copy.10), kind=kOutput, calls=%fused_computation.58 | convolution fusion | flops 331475200 | bytes 4688850 | tf_op jit(solution)/shard_map/shtlc,sta->ashcl/dot_general | solution.py:64
  57.8 3.7 %all-to-all-start = ((bf16[8,2,25600]{2,1,0:T(2,128)(2,1)}), bf16[8,2,25600]{2,1,0:T(2,128)(2,1)S(1)}, u32[]{:S(2)}, u32[]{:S(2)}) async-start(bf16[8,2,25600]{2,1,0:T(2,128)(2,1)} %reshape.583), calls=%async_computation | async-start | bytes 1638400 | tf_op jit(solution)/shard_map/all_to_all | solution.py:88
  61.7 12.7 %all-to-all-done = bf16[8,2,25600]{2,1,0:T(2,128)(2,1)S(1)} async-done(((bf16[8,2,25600]{2,1,0:T(2,128)(2,1)}), bf16[8,2,25600]{2,1,0:T(2,128)(2,1)S(1)}, u32[]{:S(2)}, u32[]{:S(2)}) %all-to-all-start) | async-done | bytes 819232 | tf_op jit(solution)/shard_map/all_to_all | solution.py:88
  75.4 2.4 copy.11
  77.8 171.5 %while.15 = (s32[]{:T(128)}, bf16[8,1,64,1616]{3,2,1,0:T(8,128)(2,1)}, bf16[8,1,200,2,2,64]{2,5,3,4,1,0:T(8,128)(2,1)}, s32[200]{0:T(256)S(1)}, s32[8,1]{0,1:T(1...) while((s32[]{:T(128)}, ...), condition=%wide.region_1.2_spmd, body=%wide.region_0.1_spmd.sunk | while | flops 175794288 | bytes 47638996 | solution.py:101
  85.2 3.5 %copy.18 = f32[1,1616,200,2]{1,2,3,0:T(8,128)} copy(f32[1,1616,200,2]{2,1,3,0:T(8,128)} %slice.24) | data formatting | bytes 5171200 | tf_op jit(solution)/shard_map/while
  90.6 3.7 %copy.19 = f32[1,1616,200,2]{1,2,3,0:T(8,128)} copy(f32[1,1616,200,2]{2,1,3,0:T(8,128)} %slice.25) | data formatting | bytes 5171200 | tf_op jit(solution)/shard_map/while
  94.5 2.5 fusion.76
  106.6 3.5 %copy.18 = f32[1,1616,200,2]{1,2,3,0:T(8,128)} copy(f32[1,1616,200,2]{2,1,3,0:T(8,128)} %slice.24) | data formatting | bytes 5171200 | tf_op jit(solution)/shard_map/while
  112.1 3.7 %copy.19 = f32[1,1616,200,2]{1,2,3,0:T(8,128)} copy(f32[1,1616,200,2]{2,1,3,0:T(8,128)} %slice.25) | data formatting | bytes 5171200 | tf_op jit(solution)/shard_map/while
  115.9 2.5 fusion.76
  128.1 3.5 %copy.18 = f32[1,1616,200,2]{1,2,3,0:T(8,128)} copy(f32[1,1616,200,2]{2,1,3,0:T(8,128)} %slice.24) | data formatting | bytes 5171200 | tf_op jit(solution)/shard_map/while
  133.5 3.7 %copy.19 = f32[1,1616,200,2]{1,2,3,0:T(8,128)} copy(f32[1,1616,200,2]{2,1,3,0:T(8,128)} %slice.25) | data formatting | bytes 5171200 | tf_op jit(solution)/shard_map/while
  137.3 2.5 fusion.76
  149.5 3.5 %copy.18 = f32[1,1616,200,2]{1,2,3,0:T(8,128)} copy(f32[1,1616,200,2]{2,1,3,0:T(8,128)} %slice.24) | data formatting | bytes 5171200 | tf_op jit(solution)/shard_map/while
  154.9 3.7 %copy.19 = f32[1,1616,200,2]{1,2,3,0:T(8,128)} copy(f32[1,1616,200,2]{2,1,3,0:T(8,128)} %slice.25) | data formatting | bytes 5171200 | tf_op jit(solution)/shard_map/while
  158.8 2.5 fusion.76
  170.9 3.5 %copy.18 = f32[1,1616,200,2]{1,2,3,0:T(8,128)} copy(f32[1,1616,200,2]{2,1,3,0:T(8,128)} %slice.24) | data formatting | bytes 5171200 | tf_op jit(solution)/shard_map/while
  176.4 3.7 %copy.19 = f32[1,1616,200,2]{1,2,3,0:T(8,128)} copy(f32[1,1616,200,2]{2,1,3,0:T(8,128)} %slice.25) | data formatting | bytes 5171200 | tf_op jit(solution)/shard_map/while
  180.2 2.5 fusion.76
  192.4 3.5 %copy.18 = f32[1,1616,200,2]{1,2,3,0:T(8,128)} copy(f32[1,1616,200,2]{2,1,3,0:T(8,128)} %slice.24) | data formatting | bytes 5171200 | tf_op jit(solution)/shard_map/while
  197.8 3.7 %copy.19 = f32[1,1616,200,2]{1,2,3,0:T(8,128)} copy(f32[1,1616,200,2]{2,1,3,0:T(8,128)} %slice.25) | data formatting | bytes 5171200 | tf_op jit(solution)/shard_map/while
  201.6 2.5 fusion.76
  213.8 3.5 %copy.18 = f32[1,1616,200,2]{1,2,3,0:T(8,128)} copy(f32[1,1616,200,2]{2,1,3,0:T(8,128)} %slice.24) | data formatting | bytes 5171200 | tf_op jit(solution)/shard_map/while
  219.2 3.7 %copy.19 = f32[1,1616,200,2]{1,2,3,0:T(8,128)} copy(f32[1,1616,200,2]{2,1,3,0:T(8,128)} %slice.25) | data formatting | bytes 5171200 | tf_op jit(solution)/shard_map/while
  223.1 2.5 fusion.76
  235.2 3.5 %copy.18 = f32[1,1616,200,2]{1,2,3,0:T(8,128)} copy(f32[1,1616,200,2]{2,1,3,0:T(8,128)} %slice.24) | data formatting | bytes 5171200 | tf_op jit(solution)/shard_map/while
  240.7 3.7 %copy.19 = f32[1,1616,200,2]{1,2,3,0:T(8,128)} copy(f32[1,1616,200,2]{2,1,3,0:T(8,128)} %slice.25) | data formatting | bytes 5171200 | tf_op jit(solution)/shard_map/while
  244.5 2.5 fusion.76
  (151 shorter events, 89.6 us)
Async XLA Ops:
  6.5 55.0 %copy-start = (s32[64]{0:T(128)S(1)}, s32[64]{0:T(128)}, u32[]{:S(2)}) copy-start(s32[64]{0:T(128)} %param.9) | copy-start | bytes 772
  6.5 43.2 %all-gather.2.cloned.1.call-start = ((), (), s32[]{:S(2)}) async-start(), calls=%async_computation.1 | async-start | bytes 2048000 | tf_op jit(solution)/shard_map/all_gather | solution.py:79
  19.4 2.4 copy-start.2
  57.8 16.6 %all-to-all-start = ((bf16[8,2,25600]{2,1,0:T(2,128)(2,1)}), bf16[8,2,25600]{2,1,0:T(2,128)(2,1)S(1)}, u32[]{:S(2)}, u32[]{:S(2)}) async-start(bf16[8,2,25600]{2,1,0:T(2,128)(2,1)} %reshape.583), calls=%async_computation | async-start | bytes 1638400 | tf_op jit(solution)/shard_map/all_to_all | solution.py:88
  90.6 3.8 %copy-start.1 = (f32[1,1616,200,2]{1,2,3,0:T(8,128)S(1)}, f32[1,1616,200,2]{1,2,3,0:T(8,128)}, u32[]{:S(2)}) copy-start(f32[1,1616,200,2]{1,2,3,0:T(8,128)} %copy.18) | copy-start | bytes 7756804 | tf_op jit(solution)/shard_map/while
  112.1 3.8 %copy-start.1 = (f32[1,1616,200,2]{1,2,3,0:T(8,128)S(1)}, f32[1,1616,200,2]{1,2,3,0:T(8,128)}, u32[]{:S(2)}) copy-start(f32[1,1616,200,2]{1,2,3,0:T(8,128)} %copy.18) | copy-start | bytes 7756804 | tf_op jit(solution)/shard_map/while
  133.5 3.8 %copy-start.1 = (f32[1,1616,200,2]{1,2,3,0:T(8,128)S(1)}, f32[1,1616,200,2]{1,2,3,0:T(8,128)}, u32[]{:S(2)}) copy-start(f32[1,1616,200,2]{1,2,3,0:T(8,128)} %copy.18) | copy-start | bytes 7756804 | tf_op jit(solution)/shard_map/while
  154.9 3.8 %copy-start.1 = (f32[1,1616,200,2]{1,2,3,0:T(8,128)S(1)}, f32[1,1616,200,2]{1,2,3,0:T(8,128)}, u32[]{:S(2)}) copy-start(f32[1,1616,200,2]{1,2,3,0:T(8,128)} %copy.18) | copy-start | bytes 7756804 | tf_op jit(solution)/shard_map/while
  176.4 3.8 %copy-start.1 = (f32[1,1616,200,2]{1,2,3,0:T(8,128)S(1)}, f32[1,1616,200,2]{1,2,3,0:T(8,128)}, u32[]{:S(2)}) copy-start(f32[1,1616,200,2]{1,2,3,0:T(8,128)} %copy.18) | copy-start | bytes 7756804 | tf_op jit(solution)/shard_map/while
  197.8 3.8 %copy-start.1 = (f32[1,1616,200,2]{1,2,3,0:T(8,128)S(1)}, f32[1,1616,200,2]{1,2,3,0:T(8,128)}, u32[]{:S(2)}) copy-start(f32[1,1616,200,2]{1,2,3,0:T(8,128)} %copy.18) | copy-start | bytes 7756804 | tf_op jit(solution)/shard_map/while
  219.2 3.8 %copy-start.1 = (f32[1,1616,200,2]{1,2,3,0:T(8,128)S(1)}, f32[1,1616,200,2]{1,2,3,0:T(8,128)}, u32[]{:S(2)}) copy-start(f32[1,1616,200,2]{1,2,3,0:T(8,128)} %copy.18) | copy-start | bytes 7756804 | tf_op jit(solution)/shard_map/while
  240.7 3.8 %copy-start.1 = (f32[1,1616,200,2]{1,2,3,0:T(8,128)S(1)}, f32[1,1616,200,2]{1,2,3,0:T(8,128)}, u32[]{:S(2)}) copy-start(f32[1,1616,200,2]{1,2,3,0:T(8,128)} %copy.18) | copy-start | bytes 7756804 | tf_op jit(solution)/shard_map/while
Sparse Core Ops, SparseCore 0:
  8.9 40.8 all-gather.1
